TPU v7x, 32 devices: a whole 2x2x4 slice. The times are simulated.
32 devices in a mesh: gx: 4 (over x, core), gy: 2 (over y), gz: 4 (over z).
Axes of the slice: x: 2, y: 2, z: 4, core: 2. Of those that a mesh axis runs over, the one named last changes fastest.
Arguments:
- fields: float32 [5, 64, 16, 512], P(None, 'gz', 'gy', 'gx'), may hold values from -4 to 4
- radius: float32 [8, 64, 16, 512], P(None, 'gz', 'gy', 'gx'), may hold values from 0.4 to 1.5
- weight: float32 [8, 64, 16, 512], P(None, 'gz', 'gy', 'gx'), may hold values from 0.05 to 0.5
- column: int32 [8, 64, 16, 512], P(None, 'gz', 'gy', 'gx'), may hold values from 0 to 127
- counts: int32 [64, 16, 512], P('gz', 'gy', 'gx'), may hold values from 1 to 8
- fall_depth: int32 [8, 64, 16, 4], P(None, 'gz', 'gy', 'gx'), may hold values from 0 to 8, as said below
Outputs:
- new_fields: float32 [5, 64, 16, 512], P(None, 'gz', 'gy', 'gx')
- moments: float32 [3, 64, 16, 512], P(None, 'gz', 'gy', 'gx')
Inputs may be any that keep to these rules, and one draw needn't show every extreme that they name: The droplet in slot s of cell (k, j, i) sits in x cell (i // 128) * 128 + column[s, k, j, i]. Slots s < counts[k, j, i] hold live droplets. The droplets of slot s in cells (k, j, b * 128) to (k, j, (b + 1) * 128 - 1) fall together by fall_depth[s, k, j, b] levels, never below the lowest level: fall_depth[s, k, j, b] <= k; 8 is reached in every draw.
All inputs are finite; a program needn't handle non-finite values. Where the computation divides by a largest or mean magnitude, that divisor is 1e-20 or more.
Results may differ from a plain program's by a relative error of at most 0.00021.
Values sent between devices are 32-bit elements; how exact they have to be, the bound alone decides.
A program may use at most 64 MiB of HBM per device.

v0:
```python
import functools
import jax
import jax.numpy as jnp
from jax import lax
from jax.experimental import pallas as pl
from jax.experimental.pallas import tpu as pltpu
from jax.sharding import PartitionSpec as P

NS = 4
FMAX = 8
SLOT_LANES = 8

sound_speed = 10.0
buoyancy = 0.5
courant_goal = 0.6
growth = 0.3

MESH = pl.DeviceIdType.MESH
FULL = {0: 0, 1: 1, 3: 2}
THIN = {2: 0, 4: 1, 5: 2, 6: 3}
AXES = ("gx", "gy", "gz")


def flux(wind, a, b, c, d, e, f):
    central = 37.0 * (c + d) - 8.0 * (b + e) + (a + f)
    upwind = 10.0 * (d - c) - 5.0 * (e - b) + (f - a)
    return wind * central - jnp.abs(wind) * upwind


def kernel(
    sizes, depth_ref, fields, radius_hbm, weight_hbm, column_hbm, counts_hbm,
    out_fields, moments, *scratch
):
    names, levels, rows, cols, slots = sizes
    refs = dict(zip(names, scratch))
    radius, weight, column, counts = (refs[n] for n in ("radius", "weight", "column", "counts"))
    send_sem, recv_sem = refs["send_sem"], refs["recv_sem"]
    shape = (rows, cols)
    lane = lax.broadcasted_iota(jnp.int32, shape, 1)
    row = lax.broadcasted_iota(jnp.int32, shape, 0)
    place = {a: lax.axis_index(a) for a in AXES}
    count = {a: lax.axis_size(a) for a in AXES}
    has_low = place["gz"] > 0
    has_high = place["gz"] < count["gz"] - 1

    def lanes_by(x, shift):
        return pltpu.roll(x, shift % cols if isinstance(shift, int) else shift, 1)

    def rows_by(x, shift):
        return pltpu.roll(x, shift % rows, 0)

    def loop(n, body, carry, unroll=True):
        return lax.fori_loop(0, n, body, carry, unroll=unroll)

    local = []
    for n, (src, dst) in enumerate(
        ((column_hbm, column), (counts_hbm, counts), (weight_hbm, weight), (radius_hbm, radius))
    ):
        copy = pltpu.make_async_copy(src, dst, refs["local_sem"].at[n])
        copy.start()
        local.append(copy)

    barrier = pltpu.get_barrier_semaphore()
    peers = 0
    for a in AXES:
        for step in range(1, count[a]):
            pl.semaphore_signal(
                barrier, inc=1,
                device_id={a: lax.rem(place[a] + step, count[a])}, device_id_type=MESH,
            )
            peers += 1

    def first(k, top):
        w = fields[4, k]
        lid = jnp.where((k == levels - 1) & jnp.logical_not(has_high), 0.0, 1.0)
        w = w * lid
        refs["W0"][k + 1] = w
        refs["C0"][k + 3] = fields[0, k]
        refs["P0"][k + 3] = fields[1, k]
        refs["U0"][k] = fields[2, k]
        refs["V0"][k] = fields[3, k]
        return jnp.maximum(top, jnp.abs(fields[2, k]) + jnp.abs(fields[3, k]) + jnp.abs(w))

    top = loop(levels, first, jnp.zeros(shape, jnp.float32))
    pl.semaphore_wait(barrier, peers)

    def max_start(phase, value):
        a = AXES[phase]
        refs["max_send"][phase] = value
        copies = []
        for step in range(1, count[a]):
            copy = pltpu.make_async_remote_copy(
                src_ref=refs["max_send"].at[phase],
                dst_ref=refs["max_recv"].at[phase, step - 1],
                send_sem=refs["max_ss"].at[phase, step - 1],
                recv_sem=refs["max_rs"].at[phase, step - 1],
                device_id={a: lax.rem(place[a] + step, count[a])}, device_id_type=MESH,
            )
            copy.start()
            copies.append(copy)
        return copies

    def max_end(phase, value, copies):
        for n, copy in enumerate(copies):
            copy.wait()
            value = jnp.maximum(value, refs["max_recv"][phase, n])
        return value

    def neighbour(a, step):
        return {a: lax.rem(place[a] + count[a] + step, count[a])}

    def copies_of(e):
        kind, at = ("f", FULL[e]) if e in FULL else ("t", THIN[e])
        out = {}
        for n, (name, a, step) in enumerate(
            (("yu", "gy", 1), ("yd", "gy", -1), ("zu", "gz", 1), ("zd", "gz", -1),
             ("xu", "gx", 1), ("xd", "gx", -1))
        ):
            out[name] = pltpu.make_async_remote_copy(
                src_ref=refs[kind + name + "_s"].at[at],
                dst_ref=refs[kind + name + "_r"].at[at],
                send_sem=send_sem.at[e, n],
                recv_sem=recv_sem.at[e, n],
                device_id=neighbour(a, step), device_id_type=MESH,
            )
        return out

    def send(e, tag):
        full = e in FULL
        kind, at = ("f", FULL[e]) if full else ("t", THIN[e])
        C, PR, U, V, W = (refs[n + tag] for n in "CPUVW")
        copies = copies_of(e)

        def pack_y(k, carry):
            p, v = PR[k + 3], V[k]
            if full:
                c = C[k + 3]
                refs["fyu_s"][at, k] = jnp.where(
                    row >= rows - 3, c, jnp.where(row == rows - 4, rows_by(v, -3), rows_by(p, -4))
                )
                refs["fyd_s"][at, k] = jnp.where(row < 3, c, rows_by(p, 3))
            else:
                refs["tyu_s"][at, pl.ds(k, 1), :] = p[rows - 1:rows]
                refs["tyu_s"][at, pl.ds(levels + k, 1), :] = v[rows - 1:rows]
                refs["tyd_s"][at, pl.ds(k, 1), :] = p[0:1]
            return carry

        loop(levels, pack_y, 0)
        width = 3 if full else 1
        for t in range(width):
            top_level = levels - width + t
            if full:
                refs["fzu_s"][at, t] = C[3 + top_level]
                refs["fzd_s"][at, t] = C[3 + t]
                refs["fzu_s"][at, 3 + t] = PR[3 + top_level]
                refs["fzd_s"][at, 3 + t] = PR[3 + t]
            else:
                refs["tzu_s"][at, 0] = PR[3 + top_level]
                refs["tzd_s"][at, 0] = PR[3]
        refs[kind + "zu_s"][at, 6 if full else 1] = W[levels]
        copies["yu"].start()
        copies["yd"].start()

        def pack_x(k, carry):
            up, down = carry
            p, u = PR[k + 3], U[k]
            if full:
                c = C[k + 3]
                high = jnp.where(
                    lane >= cols - 3, c,
                    jnp.where(lane == cols - 4, lanes_by(u, -3), lanes_by(p, -4)),
                )
                low = jnp.where(lane < 3, c, lanes_by(p, 3))
            else:
                high = jnp.where(lane == cols - 4, lanes_by(u, -3), lanes_by(p, -4))
                low = lanes_by(p, 3)
            here = lane // SLOT_LANES == k
            up = jnp.where(here, lanes_by(high, lax.rem(SLOT_LANES * (k + 1), cols)), up)
            down = jnp.where(here, lanes_by(low, SLOT_LANES * k), down)
            return up, down

        zero = jnp.zeros(shape, jnp.float32)
        up, down = loop(levels, pack_x, (zero, zero))
        refs[kind + "xu_s"][at] = up
        refs[kind + "xd_s"][at] = down

        @pl.when(has_high)
        def _():
            copies["zu"].start()

        @pl.when(has_low)
        def _():
            copies["zd"].start()

        copies["xu"].start()
        copies["xd"].start()

    def receive(e, tag):
        full = e in FULL
        kind, at = ("f", FULL[e]) if full else ("t", THIN[e])
        C, PR, W = (refs[n + tag] for n in "CPW")
        copies = copies_of(e)
        width = 3 if full else 1

        copies["xu"].wait()
        copies["xd"].wait()
        up, down = refs[kind + "xu_r"][at], refs[kind + "xd_r"][at]

        def unpack_x(k, carry):
            low = lanes_by(up, cols - SLOT_LANES * (k + 1))
            high = lanes_by(down, (cols - SLOT_LANES * k) % cols)
            if full:
                refs["HXC" + tag][k] = jnp.where(lane >= cols - 3, low, high)
            refs["HXP" + tag][k] = jnp.where(lane >= cols - 3, lanes_by(low, 4), lanes_by(high, -3))
            refs["HXU" + tag][k] = lanes_by(low, 3)
            return carry

        loop(levels, unpack_x, 0)

        @pl.when(has_high)
        def _():
            copies["zu"].wait_send()
            copies["zd"].wait_recv()
            for t in range(width):
                if full:
                    C[3 + levels + t] = refs["fzd_r"][at, t]
                    PR[3 + levels + t] = refs["fzd_r"][at, 3 + t]
                else:
                    PR[3 + levels + t] = refs["tzd_r"][at, t]

        @pl.when(jnp.logical_not(has_high))
        def _():
            for t in range(width):
                if full:
                    C[3 + levels + t] = jnp.zeros(shape, jnp.float32)
                PR[3 + levels + t] = jnp.zeros(shape, jnp.float32)

        @pl.when(has_low)
        def _():
            copies["zd"].wait_send()
            copies["zu"].wait_recv()
            for t in range(width):
                if full:
                    C[t] = refs["fzu_r"][at, t]
                    PR[t] = refs["fzu_r"][at, 3 + t]
                else:
                    PR[2] = refs["tzu_r"][at, 0]
            W[0] = refs[kind + "zu_r"][at, 6 if full else 1]

        @pl.when(jnp.logical_not(has_low))
        def _():
            for t in range(width):
                if full:
                    C[t] = jnp.zeros(shape, jnp.float32)
                PR[3 - width + t] = jnp.zeros(shape, jnp.float32)
            W[0] = jnp.zeros(shape, jnp.float32)

        copies["yu"].wait()
        copies["yd"].wait()

        def unpack_y(k, carry):
            if full:
                low, high = refs["fyu_r"][at, k], refs["fyd_r"][at, k]
                refs["HYC" + tag][k] = jnp.where(row >= rows - 3, low, high)
                refs["HYP" + tag][k] = jnp.where(row >= rows - 3, rows_by(low, 4), rows_by(high, -3))
                refs["HYV" + tag][k] = rows_by(low, 3)
            else:
                low = refs["tyu_r"][at, pl.ds(k, 1), :]
                high = refs["tyd_r"][at, pl.ds(k, 1), :]
                refs["HYP" + tag][k] = jnp.where(row == rows - 1, low, high)
                refs["HYV" + tag][k] = jnp.broadcast_to(
                    refs["tyu_r"][at, pl.ds(levels + k, 1), :], shape
                )
            return carry

        loop(levels, unpack_y, 0)

    def sides(q, halo, by, index, extent):
        low = [by(jnp.where(index >= extent - n, halo, q), n) for n in (3, 2, 1)]
        high = [by(jnp.where(index < n, halo, q), -n) for n in (1, 2, 3)]
        return (*low, q, *high)

    def advect(tag):
        U, V, W = (refs[n + tag] for n in "UVW")

        def level(k, carry):
            u, v, w, w_low = U[k], V[k], W[k + 1], W[k]
            u_low = lanes_by(jnp.where(lane == cols - 1, refs["HXU" + tag][k], u), 1)
            v_low = rows_by(jnp.where(row == rows - 1, refs["HYV" + tag][k], v), 1)
            for name, rate in (("C", "rate_c"), ("P", "rate_p")):
                Q = refs[name + tag]
                q = Q[k + 3]
                xs = sides(q, refs["HX" + name + tag][k], lanes_by, lane, cols)
                ys = sides(q, refs["HY" + name + tag][k], rows_by, row, rows)
                zs = [Q[k + n] for n in range(7)]
                total = flux(u, *xs[1:]) - flux(u_low, *xs[:6])
                total = total + (flux(v, *ys[1:]) - flux(v_low, *ys[:6]))
                total = total + (flux(w, *zs[1:]) - flux(w_low, *zs[:6]))
                refs[rate][k] = total * (-1.0 / 60.0)
            return carry

        loop(levels, level, 0, 4)
        C = refs["C" + tag]
        lid_low = jnp.where(has_low, 1.0, 0.0)
        lid_high = jnp.where(has_high, 1.0, 0.0)
        for k in range(levels + 1):
            lift = (buoyancy * 0.5) * (C[k + 2] + C[k + 3])
            if k == 0:
                lift = lift * lid_low
            if k == levels:
                lift = lift * lid_high
            refs["lift"][k] = lift

    def substep(source, sub_step):
        SP, SU, SV, SW = (refs[n + source] for n in "PUVW")
        HXP, HXU, HYP, HYV = (refs[n + source] for n in ("HXP", "HXU", "HYP", "HYV"))
        DP, DU, DV, DW = (refs[n + "1"] for n in "PUVW")
        push = sub_step * sound_speed
        lid_low = jnp.where(has_low, 1.0, 0.0)

        def vertical(k):
            return SW[k] + sub_step * (
                refs["lift"][k] - sound_speed * (SP[k + 3] - SP[k + 2])
            )

        def level(k, w_low):
            p, u, v = SP[k + 3], SU[k], SV[k]
            hx, hy = HXP[k], HYP[k]
            lid = jnp.where((k == levels - 1) & jnp.logical_not(has_high), 0.0, 1.0)
            w = vertical(k + 1) * lid
            px = lanes_by(p, -1)
            py = rows_by(p, -1)
            u_new = u - push * (jnp.where(lane == cols - 1, lanes_by(hx, -1), px) - p)
            v_new = v - push * (jnp.where(row == rows - 1, rows_by(hy, -1), py) - p)
            u_halo = HXU[k] - push * (px - hx)
            v_halo = HYV[k] - push * (py - hy)
            u_low = lanes_by(jnp.where(lane == cols - 1, u_halo, u_new), 1)
            v_low = rows_by(jnp.where(row == rows - 1, v_halo, v_new), 1)
            div = (u_new - u_low) + (v_new - v_low) + (w - w_low)
            DU[k] = u_new
            DV[k] = v_new
            DW[k + 1] = w
            DP[k + 3] = p + sub_step * (refs["rate_p"][k] - sound_speed * div)
            return w

        loop(levels, level, vertical(0) * lid_low)

    def tracer(scale):
        def level(k, carry):
            refs["C1"][k + 3] = refs["C0"][k + 3] + scale * refs["rate_c"][k]
            return carry

        loop(levels, level, 0)

    acc, vals = refs["acc"], refs["vals"]

    def growth_terms():
        for n in range(4):
            local[n].wait()

        def cell(k, carry):
            c = refs["C1"][k + 3]
            live = counts[k]
            for s in range(slots):
                near = jnp.take_along_axis(c, column[s, k], axis=1, mode="promise_in_bounds")
                r = radius[s, k]
                squared = r * r * jnp.exp(growth * near)
                number = jnp.where(live > s, weight[s, k], 0.0)
                area = number * squared
                mass = area * jnp.sqrt(squared)
                for m, term in enumerate((number, area, mass)):
                    high = term.astype(jnp.bfloat16).astype(jnp.float32)
                    vals[s, k, m * rows:(m + 1) * rows, :] = high
                    vals[s, k, (m + 3) * rows:(m + 4) * rows, :] = term - high
                vals[s, k, 6 * rows:, :] = jnp.zeros((2 * rows, cols), jnp.float32)
            return carry

        loop(levels, cell, 0, 2)

    def clear():
        def level(k, carry):
            acc[k] = jnp.zeros((8 * rows, cols), jnp.float32)
            return carry

        loop(levels + FMAX, level, 0)

    def deposit(begin, end):
        ids = lax.broadcasted_iota(jnp.int32, (cols, cols), 0).astype(jnp.float32).astype(jnp.bfloat16)
        one = jnp.ones((cols, cols), jnp.bfloat16)
        none = jnp.zeros((cols, cols), jnp.bfloat16)
        zero = jnp.zeros((8, cols), jnp.float32)

        def cell(n, carry):
            k, j = begin + n // rows, n % rows
            by_depth = [None] * (FMAX + 1)
            for s in range(0, slots, 2):
                left, right, hots = [], [], []
                for t in range(2):
                    v = vals[s + t, k, pl.ds(j, 8, stride=rows), :]
                    left.append(v if t == 0 else zero)
                    right.append(zero if t == 0 else v)
                    c = column[s + t, k, pl.ds(j, 1), :].astype(jnp.float32).astype(jnp.bfloat16)
                    hots.append(jnp.where(ids == jnp.broadcast_to(c, (cols, cols)), one, none))
                lhs = jnp.concatenate(
                    [jnp.concatenate(left, axis=0), jnp.concatenate(right, axis=0)], axis=1
                ).astype(jnp.bfloat16)
                rhs = jnp.concatenate(hots, axis=1)
                got = lax.dot_general(
                    lhs, rhs, (((1,), (1,)), ((), ())), preferred_element_type=jnp.float32
                )
                for t in range(2):
                    part = got[8 * t:8 * (t + 1)]
                    depth = depth_ref[s + t, k * rows + j]
                    for d in range(FMAX + 1):
                        term = jnp.where(depth == d, part, 0.0)
                        by_depth[d] = term if by_depth[d] is None else by_depth[d] + term
            for d in range(FMAX + 1):
                at = pl.ds(pl.multiple_of(j * 8, 8), 8)
                acc[k + FMAX - d, at, :] = acc[k + FMAX - d, at, :] + by_depth[d]
            return carry

        lax.fori_loop(0, (end - begin) * rows, cell, 0, unroll=2)

    def collect(m, l):
        return acc[l, pl.ds(m, rows, stride=8), :] + acc[l, pl.ds(m + 3, rows, stride=8), :]

    copies = max_start(0, top)
    send(0, "0")
    top = max_end(0, top, copies)
    copies = max_start(1, top)
    top = max_end(1, top, copies)
    copies = max_start(2, top)
    clear()
    receive(0, "0")
    advect("0")
    top = max_end(2, top, copies)
    time_step = courant_goal / (1.0 + jnp.max(top, axis=(0, 1), keepdims=True))
    time_step = jnp.broadcast_to(time_step, shape)

    third = time_step * (1.0 / 3.0)
    tracer(third)
    substep("0", third)
    send(1, "1")
    receive(1, "1")
    advect("1")
    half = time_step * 0.5
    tracer(half)
    part = half / (NS // 2)
    substep("0", part)
    send(2, "1")
    receive(2, "1")
    substep("1", part)
    send(3, "1")
    receive(3, "1")
    advect("1")
    tracer(time_step)
    part = time_step / NS
    substep("0", part)
    send(4, "1")
    growth_terms()
    receive(4, "1")
    substep("1", part)
    send(5, "1")
    deposit(0, FMAX)
    moment_copy = pltpu.make_async_remote_copy(
        src_ref=refs["fall_s"], dst_ref=refs["fall_r"],
        send_sem=refs["fall_sem"].at[0], recv_sem=refs["fall_sem"].at[1],
        device_id=neighbour("gz", -1), device_id_type=MESH,
    )
    for m in range(3):
        for l in range(FMAX):
            refs["fall_s"][m, l] = collect(m, l)

    receive(5, "1")

    @pl.when(has_low)
    def _():
        moment_copy.start()

    substep("1", part)
    send(6, "1")
    deposit(FMAX, levels)
    receive(6, "1")
    substep("1", part)

    def write(k, carry):
        out_fields[0, k] = refs["C1"][k + 3]
        out_fields[1, k] = refs["P1"][k + 3]
        out_fields[2, k] = refs["U1"][k]
        out_fields[3, k] = refs["V1"][k]
        out_fields[4, k] = refs["W1"][k + 1]
        return carry

    loop(levels, write, 0)
    for m in range(3):
        for l in range(levels):
            moments[m, l] = collect(m, l + FMAX)

    @pl.when(has_low)
    def _():
        moment_copy.wait_send()

    @pl.when(has_high)
    def _():
        moment_copy.wait_recv()
        for m in range(3):
            for l in range(FMAX):
                at = levels - FMAX + l
                moments[m, at] = moments[m, at] + refs["fall_r"][m, l]


def per_device(fields, radius, weight, column, counts, fall_depth):
    levels, rows, cols = fields.shape[1:]
    slots = radius.shape[0]
    assert levels * SLOT_LANES <= cols and rows == 8 and FMAX <= levels
    f32 = jnp.float32
    cell = (rows, cols)
    widest = max(lax.axis_size(a) for a in AXES) - 1
    spaces = {}

    def add(name, *shape, dtype=f32):
        spaces[name] = pltpu.VMEM(shape, dtype)

    add("radius", *radius.shape)
    add("weight", *weight.shape)
    add("column", *column.shape, dtype=jnp.int32)
    add("counts", *counts.shape, dtype=jnp.int32)
    for tag in "01":
        add("C" + tag, levels + 6, *cell)
        add("P" + tag, levels + 6, *cell)
        add("U" + tag, levels, *cell)
        add("V" + tag, levels, *cell)
        add("W" + tag, levels + 1, *cell)
        for name in ("HXC", "HXP", "HXU", "HYC", "HYP", "HYV"):
            add(name + tag, levels, *cell)
    add("rate_c", levels, *cell)
    add("rate_p", levels, *cell)
    add("lift", levels + 1, *cell)
    add("max_send", 3, *cell)
    add("max_recv", 3, widest, *cell)
    for end in ("_s", "_r"):
        for name, shape in (
            ("fxu", cell), ("fxd", cell), ("fyu", (levels,) + cell), ("fyd", (levels,) + cell),
            ("fzu", (7,) + cell), ("fzd", (6,) + cell),
        ):
            add(name + end, len(FULL), *shape)
        for name, shape in (
            ("txu", cell), ("txd", cell), ("tyu", (2 * levels, cols)), ("tyd", (levels, cols)),
            ("tzu", (2,) + cell), ("tzd", (1,) + cell),
        ):
            add(name + end, len(THIN), *shape)
    add("acc", levels + FMAX, 8 * rows, cols)
    add("vals", slots, levels, 8 * rows, cols)
    add("fall_s", 3, FMAX, *cell)
    add("fall_r", 3, FMAX, *cell)
    rounds = len(FULL) + len(THIN)
    spaces["send_sem"] = pltpu.SemaphoreType.DMA((rounds, 6))
    spaces["recv_sem"] = pltpu.SemaphoreType.DMA((rounds, 6))
    spaces["max_ss"] = pltpu.SemaphoreType.DMA((3, widest))
    spaces["max_rs"] = pltpu.SemaphoreType.DMA((3, widest))
    spaces["fall_sem"] = pltpu.SemaphoreType.DMA((2,))
    spaces["local_sem"] = pltpu.SemaphoreType.DMA((4,))
    vmem = pl.BlockSpec(memory_space=pltpu.VMEM)
    anywhere = pl.BlockSpec(memory_space=pl.ANY)
    return pl.pallas_call(
        functools.partial(kernel, (tuple(spaces), levels, rows, cols, slots)),
        out_shape=(
            jax.ShapeDtypeStruct(fields.shape, f32),
            jax.ShapeDtypeStruct((3, levels, rows, cols), f32),
        ),
        in_specs=[pl.BlockSpec(memory_space=pltpu.SMEM), vmem] + [anywhere] * 4,
        out_specs=(vmem, vmem),
        scratch_shapes=list(spaces.values()),
        compiler_params=pltpu.CompilerParams(
            collective_id=0, has_side_effects=True, vmem_limit_bytes=48 * 1024 * 1024
        ),
        name="slab_step",
    )(fall_depth.reshape(slots, levels * rows), fields, radius, weight, column, counts)


def solution(mesh):
    in_specs = (
        P(None, "gz", "gy", "gx"),
        P(None, "gz", "gy", "gx"),
        P(None, "gz", "gy", "gx"),
        P(None, "gz", "gy", "gx"),
        P("gz", "gy", "gx"),
        P(None, "gz", "gy", "gx"),
    )
    out_specs = (P(None, "gz", "gy", "gx"), P(None, "gz", "gy", "gx"))
    return jax.shard_map(
        per_device, mesh=mesh, in_specs=in_specs, out_specs=out_specs, check_vma=False
    )
```

profile of v0, /device:TPU:0, one launch (start us, length us, event | category | flops | bytes accessed | tf_op | source)
XLA Modules:
  0.0 58.1 jit_solution(9140372260415382188)
XLA Ops:
  0.6 0.0 copy-start.4
  0.6 0.9 %copy.9 = s32[8,16,8,1]{2,1,0,3:T(8,128)S(1)} copy(s32[8,16,8,1]{1,3,2,0:T(1,128)} %param.11) | data formatting | bytes 8192 | tf_op args[5]
  1.5 0.1 reshape.7.depth_ref
  1.6 0.0 copy-done.4
  1.6 0.0 copy-start
  1.6 1.0 %copy-done = f32[8,16,8,128]{3,2,1,0:T(8,128)S(1)} copy-done((f32[8,16,8,128]{3,2,1,0:T(8,128)S(1)}, f32[8,16,8,128]{3,2,1,0:T(8,128)}, u32[]{:S(2)}) %copy-start) | copy-done | bytes 524312
  2.7 0.0 copy-start.1
  2.7 1.0 %copy-done.1 = f32[8,16,8,128]{3,2,1,0:T(8,128)S(1)} copy-done((f32[8,16,8,128]{3,2,1,0:T(8,128)S(1)}, f32[8,16,8,128]{3,2,1,0:T(8,128)}, u32[]{:S(2)}) %copy-start.1) | copy-done | bytes 524312
  3.7 0.0 copy-start.2
  3.7 1.0 %copy-done.2 = s32[8,16,8,128]{3,2,1,0:T(8,128)S(1)} copy-done((s32[8,16,8,128]{3,2,1,0:T(8,128)S(1)}, s32[8,16,8,128]{3,2,1,0:T(8,128)}, u32[]{:S(2)}) %copy-start.2) | copy-done | bytes 524312
  4.7 0.0 copy-start.3
  4.7 1.0 %copy-done.3 = f32[5,16,8,128]{3,2,1,0:T(8,128)S(1)} copy-done((f32[5,16,8,128]{3,2,1,0:T(8,128)S(1)}, f32[5,16,8,128]{3,2,1,0:T(8,128)}, u32[]{:S(2)}) %copy-start.3) | copy-done | bytes 327704
  5.7 50.9 %slab_step.1 = (f32[5,16,8,128]{3,2,1,0:T(8,128)S(1)}, f32[3,16,8,128]{3,2,1,0:T(8,128)S(1)}) custom-call(s32[8,128]{1,0:T(8,128)S(1)} %reshape.7.depth_ref, f32[5,16,8,128]{3,2,1,0:T(8,128)S(1)} %copy-done.3, f32[8,16,8,128]{3,2,1,0:T(8,128)S(1)} %copy-done, f32[8,16,8,128]{3,2,1,0:T(8,128)S(1)} %copy-done.1, s32[8,16,8,128]{3,2,1,0:T(8,128)S(1)} %copy-done.2, ...), custom_call_target="tpu_custom_call" | custom-call | tf_op jit(solution)/shard_map/slab_step/pallas_call | solution.py:565
  56.7 0.7 %copy.12 = f32[5,16,8,128]{3,2,1,0:T(8,128)} copy(f32[5,16,8,128]{3,2,1,0:T(8,128)S(1)} %get-tuple-element.4) | data formatting | bytes 655360
  57.4 0.7 %copy.13 = f32[3,16,8,128]{3,2,1,0:T(8,128)} copy(f32[3,16,8,128]{3,2,1,0:T(8,128)S(1)} %get-tuple-element.5) | data formatting | bytes 393216
Async XLA Ops:
  0.6 1.0 %copy-start.4 = (s32[16,8,128]{2,1,0:T(8,128)S(1)}, s32[16,8,128]{2,1,0:T(8,128)}, u32[]{:S(2)}) copy-start(s32[16,8,128]{2,1,0:T(8,128)} %counts_hbm.1) | copy-start | bytes 196612
  1.6 1.0 %copy-start = (f32[8,16,8,128]{3,2,1,0:T(8,128)S(1)}, f32[8,16,8,128]{3,2,1,0:T(8,128)}, u32[]{:S(2)}) copy-start(f32[8,16,8,128]{3,2,1,0:T(8,128)} %radius_hbm.1) | copy-start | bytes 1572868
  2.7 1.0 %copy-start.1 = (f32[8,16,8,128]{3,2,1,0:T(8,128)S(1)}, f32[8,16,8,128]{3,2,1,0:T(8,128)}, u32[]{:S(2)}) copy-start(f32[8,16,8,128]{3,2,1,0:T(8,128)} %weight_hbm.1) | copy-start | bytes 1572868
  3.7 1.0 %copy-start.2 = (s32[8,16,8,128]{3,2,1,0:T(8,128)S(1)}, s32[8,16,8,128]{3,2,1,0:T(8,128)}, u32[]{:S(2)}) copy-start(s32[8,16,8,128]{3,2,1,0:T(8,128)} %column_hbm.1) | copy-start | bytes 1572868
  4.7 1.0 %copy-start.3 = (f32[5,16,8,128]{3,2,1,0:T(8,128)S(1)}, f32[5,16,8,128]{3,2,1,0:T(8,128)}, u32[]{:S(2)}) copy-start(f32[5,16,8,128]{3,2,1,0:T(8,128)} %fields.1) | copy-start | bytes 983044
where the time goes:
time: 58.4 us; the launch traced here: 58.1 us
  Pallas kernels  50.9 us (87%)
  local copies, waits for them, and re-layouts  6.46 us (11%)
  between operations  0.67 us (1%)
    pallas_call x1, Pallas kernels, per_device(): pl.pallas_call(functools.partial(kernel, (tuple(spaces), levels, rows, co...  50.9 us
    unnamed x13, local copies, waits for them, and re-layouts  6.36 us

commit v1 on v0

--- a/solution.py
+++ b/solution.py
@@ -8,6 +8,7 @@
 
 NS = 4
 FMAX = 8
+CELLS = 8
 SLOT_LANES = 8
 
 sound_speed = 10.0
@@ -18,7 +19,7 @@
 MESH = pl.DeviceIdType.MESH
 FULL = {0: 0, 1: 1, 3: 2}
 THIN = {2: 0, 4: 1, 5: 2, 6: 3}
-AXES = ("gx", "gy", "gz")
+AXES = ("gy", "gx", "gz")
 
 
 def flux(wind, a, b, c, d, e, f):
@@ -28,12 +29,13 @@
 
 
 def kernel(
-    sizes, depth_ref, fields, radius_hbm, weight_hbm, column_hbm, counts_hbm,
+    sizes, depth_ref, fields_hbm, radius_hbm, weight_hbm, column_hbm, counts_hbm,
     out_fields, moments, *scratch
 ):
     names, levels, rows, cols, slots = sizes
     refs = dict(zip(names, scratch))
     radius, weight, column, counts = (refs[n] for n in ("radius", "weight", "column", "counts"))
+    fields = refs["fields"]
     send_sem, recv_sem = refs["send_sem"], refs["recv_sem"]
     shape = (rows, cols)
     lane = lax.broadcasted_iota(jnp.int32, shape, 1)
@@ -52,6 +54,8 @@
     def loop(n, body, carry, unroll=True):
         return lax.fori_loop(0, n, body, carry, unroll=unroll)
 
+    fields_copy = pltpu.make_async_copy(fields_hbm, fields, refs["local_sem"].at[4])
+    fields_copy.start()
     local = []
     for n, (src, dst) in enumerate(
         ((column_hbm, column), (counts_hbm, counts), (weight_hbm, weight), (radius_hbm, radius))
@@ -69,6 +73,8 @@
                 device_id={a: lax.rem(place[a] + step, count[a])}, device_id_type=MESH,
             )
             peers += 1
+
+    fields_copy.wait()
 
     def first(k, top):
         w = fields[4, k]
@@ -109,13 +115,15 @@
     def neighbour(a, step):
         return {a: lax.rem(place[a] + count[a] + step, count[a])}
 
-    def copies_of(e):
+    def copies_of(e, wanted=("yu", "yd", "zu", "zd", "xu", "xd")):
         kind, at = ("f", FULL[e]) if e in FULL else ("t", THIN[e])
         out = {}
         for n, (name, a, step) in enumerate(
             (("yu", "gy", 1), ("yd", "gy", -1), ("zu", "gz", 1), ("zd", "gz", -1),
              ("xu", "gx", 1), ("xd", "gx", -1))
         ):
+            if name not in wanted:
+                continue
             out[name] = pltpu.make_async_remote_copy(
                 src_ref=refs[kind + name + "_s"].at[at],
                 dst_ref=refs[kind + name + "_r"].at[at],
@@ -199,7 +207,7 @@
         full = e in FULL
         kind, at = ("f", FULL[e]) if full else ("t", THIN[e])
         C, PR, W = (refs[n + tag] for n in "CPW")
-        copies = copies_of(e)
+        copies = copies_of(e, ("xu", "xd", "zu", "zd"))
         width = 3 if full else 1
 
         copies["xu"].wait()
@@ -255,6 +263,10 @@
                 PR[3 - width + t] = jnp.zeros(shape, jnp.float32)
             W[0] = jnp.zeros(shape, jnp.float32)
 
+    def receive_y(e, tag):
+        full = e in FULL
+        at = FULL[e] if full else THIN[e]
+        copies = copies_of(e, ("yu", "yd"))
         copies["yu"].wait()
         copies["yd"].wait()
 
@@ -280,26 +292,33 @@
         high = [by(jnp.where(index < n, halo, q), -n) for n in (1, 2, 3)]
         return (*low, q, *high)
 
-    def advect(tag):
+    def advect(tag, along_y):
         U, V, W = (refs[n + tag] for n in "UVW")
 
         def level(k, carry):
-            u, v, w, w_low = U[k], V[k], W[k + 1], W[k]
+            u, w, w_low = U[k], W[k + 1], W[k]
             u_low = lanes_by(jnp.where(lane == cols - 1, refs["HXU" + tag][k], u), 1)
+            for name, rate in (("C", "rate_c"), ("P", "rate_p")):
+                Q = refs[name + tag]
+                xs = sides(Q[k + 3], refs["HX" + name + tag][k], lanes_by, lane, cols)
+                zs = [Q[k + n] for n in range(7)]
+                total = flux(u, *xs[1:]) - flux(u_low, *xs[:6])
+                refs[rate][k] = total + (flux(w, *zs[1:]) - flux(w_low, *zs[:6]))
+            return carry
+
+        def level_y(k, carry):
+            v = V[k]
             v_low = rows_by(jnp.where(row == rows - 1, refs["HYV" + tag][k], v), 1)
             for name, rate in (("C", "rate_c"), ("P", "rate_p")):
-                Q = refs[name + tag]
-                q = Q[k + 3]
-                xs = sides(q, refs["HX" + name + tag][k], lanes_by, lane, cols)
-                ys = sides(q, refs["HY" + name + tag][k], rows_by, row, rows)
-                zs = [Q[k + n] for n in range(7)]
-                total = flux(u, *xs[1:]) - flux(u_low, *xs[:6])
-                total = total + (flux(v, *ys[1:]) - flux(v_low, *ys[:6]))
-                total = total + (flux(w, *zs[1:]) - flux(w_low, *zs[:6]))
+                ys = sides(refs[name + tag][k + 3], refs["HY" + name + tag][k], rows_by, row, rows)
+                total = refs[rate][k] + (flux(v, *ys[1:]) - flux(v_low, *ys[:6]))
                 refs[rate][k] = total * (-1.0 / 60.0)
             return carry
 
-        loop(levels, level, 0, 4)
+        if along_y:
+            loop(levels, level_y, 0, 8)
+            return
+        loop(levels, level, 0, 8)
         C = refs["C" + tag]
         lid_low = jnp.where(has_low, 1.0, 0.0)
         lid_high = jnp.where(has_high, 1.0, 0.0)
@@ -393,23 +412,23 @@
         def cell(n, carry):
             k, j = begin + n // rows, n % rows
             by_depth = [None] * (FMAX + 1)
-            for s in range(0, slots, 2):
-                left, right, hots = [], [], []
-                for t in range(2):
+            for s in range(0, slots, 4):
+                left, hots = [], []
+                for t in range(4):
                     v = vals[s + t, k, pl.ds(j, 8, stride=rows), :]
-                    left.append(v if t == 0 else zero)
-                    right.append(zero if t == 0 else v)
+                    left.append(jnp.concatenate([v, zero] if t % 2 == 0 else [zero, v], axis=1))
                     c = column[s + t, k, pl.ds(j, 1), :].astype(jnp.float32).astype(jnp.bfloat16)
                     hots.append(jnp.where(ids == jnp.broadcast_to(c, (cols, cols)), one, none))
-                lhs = jnp.concatenate(
-                    [jnp.concatenate(left, axis=0), jnp.concatenate(right, axis=0)], axis=1
-                ).astype(jnp.bfloat16)
-                rhs = jnp.concatenate(hots, axis=1)
+                lhs = jnp.concatenate(left, axis=0).astype(jnp.bfloat16)
+                rhs = jnp.concatenate(
+                    [jnp.concatenate(hots[:2], axis=1), jnp.concatenate(hots[2:], axis=1)], axis=0
+                )
                 got = lax.dot_general(
                     lhs, rhs, (((1,), (1,)), ((), ())), preferred_element_type=jnp.float32
                 )
-                for t in range(2):
-                    part = got[8 * t:8 * (t + 1)]
+                for t in range(4):
+                    half = t // 2
+                    part = got[8 * t:8 * (t + 1), half * cols:(half + 1) * cols]
                     depth = depth_ref[s + t, k * rows + j]
                     for d in range(FMAX + 1):
                         term = jnp.where(depth == d, part, 0.0)
@@ -419,7 +438,7 @@
                 acc[k + FMAX - d, at, :] = acc[k + FMAX - d, at, :] + by_depth[d]
             return carry
 
-        lax.fori_loop(0, (end - begin) * rows, cell, 0, unroll=2)
+        lax.fori_loop(0, (end - begin) * rows, cell, 0, unroll=CELLS)
 
     def collect(m, l):
         return acc[l, pl.ds(m, rows, stride=8), :] + acc[l, pl.ds(m + 3, rows, stride=8), :]
@@ -432,7 +451,9 @@
     copies = max_start(2, top)
     clear()
     receive(0, "0")
-    advect("0")
+    advect("0", False)
+    receive_y(0, "0")
+    advect("0", True)
     top = max_end(2, top, copies)
     time_step = courant_goal / (1.0 + jnp.max(top, axis=(0, 1), keepdims=True))
     time_step = jnp.broadcast_to(time_step, shape)
@@ -442,23 +463,29 @@
     substep("0", third)
     send(1, "1")
     receive(1, "1")
-    advect("1")
+    advect("1", False)
+    receive_y(1, "1")
+    advect("1", True)
     half = time_step * 0.5
     tracer(half)
     part = half / (NS // 2)
     substep("0", part)
     send(2, "1")
     receive(2, "1")
+    receive_y(2, "1")
     substep("1", part)
     send(3, "1")
     receive(3, "1")
-    advect("1")
+    advect("1", False)
+    receive_y(3, "1")
+    advect("1", True)
     tracer(time_step)
     part = time_step / NS
     substep("0", part)
     send(4, "1")
     growth_terms()
     receive(4, "1")
+    receive_y(4, "1")
     substep("1", part)
     send(5, "1")
     deposit(0, FMAX)
@@ -472,6 +499,7 @@
             refs["fall_s"][m, l] = collect(m, l)
 
     receive(5, "1")
+    receive_y(5, "1")
 
     @pl.when(has_low)
     def _():
@@ -481,6 +509,7 @@
     send(6, "1")
     deposit(FMAX, levels)
     receive(6, "1")
+    receive_y(6, "1")
     substep("1", part)
 
     def write(k, carry):
@@ -512,7 +541,7 @@
 def per_device(fields, radius, weight, column, counts, fall_depth):
     levels, rows, cols = fields.shape[1:]
     slots = radius.shape[0]
-    assert levels * SLOT_LANES <= cols and rows == 8 and FMAX <= levels
+    assert slots % 4 == 0 and levels * SLOT_LANES <= cols and rows == 8 and FMAX <= levels
     f32 = jnp.float32
     cell = (rows, cols)
     widest = max(lax.axis_size(a) for a in AXES) - 1
@@ -521,6 +550,7 @@
     def add(name, *shape, dtype=f32):
         spaces[name] = pltpu.VMEM(shape, dtype)
 
+    add("fields", *fields.shape)
     add("radius", *radius.shape)
     add("weight", *weight.shape)
     add("column", *column.shape, dtype=jnp.int32)
@@ -559,16 +589,16 @@
     spaces["max_ss"] = pltpu.SemaphoreType.DMA((3, widest))
     spaces["max_rs"] = pltpu.SemaphoreType.DMA((3, widest))
     spaces["fall_sem"] = pltpu.SemaphoreType.DMA((2,))
-    spaces["local_sem"] = pltpu.SemaphoreType.DMA((4,))
+    spaces["local_sem"] = pltpu.SemaphoreType.DMA((5,))
     vmem = pl.BlockSpec(memory_space=pltpu.VMEM)
-    anywhere = pl.BlockSpec(memory_space=pl.ANY)
+    anywhere = pl.BlockSpec(memory_space=pltpu.HBM)
     return pl.pallas_call(
         functools.partial(kernel, (tuple(spaces), levels, rows, cols, slots)),
         out_shape=(
             jax.ShapeDtypeStruct(fields.shape, f32),
             jax.ShapeDtypeStruct((3, levels, rows, cols), f32),
         ),
-        in_specs=[pl.BlockSpec(memory_space=pltpu.SMEM), vmem] + [anywhere] * 4,
+        in_specs=[pl.BlockSpec(memory_space=pltpu.SMEM)] + [anywhere] * 5,
         out_specs=(vmem, vmem),
         scratch_shapes=list(spaces.values()),
         compiler_params=pltpu.CompilerParams(

time: 58.4 us -> 54.6 us (0.935)
  Pallas kernels: 50.9 us -> 47.1 us
    pallas_call x1, Pallas kernels: 50.9 us -> 47.1 us  [per_device(): pl.pallas_call(functools.partial(kernel, (tuple(spaces), levels, rows, co...]
where the time goes in v1:
time: 54.6 us; the launch traced here: 54.2 us
  Pallas kernels  47.1 us (86%)
  local copies, waits for them, and re-layouts  6.46 us (12%)
  between operations  0.67 us (1%)
    pallas_call x1, Pallas kernels, per_device(): pl.pallas_call(functools.partial(kernel, (tuple(spaces), levels, rows, co...  47.1 us
    unnamed x13, local copies, waits for them, and re-layouts  6.36 us

profile of v1, /device:TPU:0, one launch (start us, length us, event | category | flops | bytes accessed | tf_op | source)
XLA Modules:
  0.0 54.2 jit_solution(11721475607268897502)
XLA Ops:
  0.6 0.0 copy-start.4
  0.6 0.9 %copy.9 = s32[8,16,8,1]{2,1,0,3:T(8,128)S(1)} copy(s32[8,16,8,1]{1,3,2,0:T(1,128)} %param.11) | data formatting | bytes 8192 | tf_op args[5]
  1.5 0.1 reshape.7.depth_ref
  1.6 0.0 copy-done.4
  1.6 0.0 copy-start
  1.6 1.0 %copy-done = f32[8,16,8,128]{3,2,1,0:T(8,128)S(1)} copy-done((f32[8,16,8,128]{3,2,1,0:T(8,128)S(1)}, f32[8,16,8,128]{3,2,1,0:T(8,128)}, u32[]{:S(2)}) %copy-start) | copy-done | bytes 524312
  2.7 0.0 copy-start.1
  2.7 1.0 %copy-done.1 = f32[8,16,8,128]{3,2,1,0:T(8,128)S(1)} copy-done((f32[8,16,8,128]{3,2,1,0:T(8,128)S(1)}, f32[8,16,8,128]{3,2,1,0:T(8,128)}, u32[]{:S(2)}) %copy-start.1) | copy-done | bytes 524312
  3.7 0.0 copy-start.2
  3.7 1.0 %copy-done.2 = s32[8,16,8,128]{3,2,1,0:T(8,128)S(1)} copy-done((s32[8,16,8,128]{3,2,1,0:T(8,128)S(1)}, s32[8,16,8,128]{3,2,1,0:T(8,128)}, u32[]{:S(2)}) %copy-start.2) | copy-done | bytes 524312
  4.7 0.0 copy-start.3
  4.7 1.0 %copy-done.3 = f32[5,16,8,128]{3,2,1,0:T(8,128)S(1)} copy-done((f32[5,16,8,128]{3,2,1,0:T(8,128)S(1)}, f32[5,16,8,128]{3,2,1,0:T(8,128)}, u32[]{:S(2)}) %copy-start.3) | copy-done | bytes 327704
  5.7 47.1 %slab_step.1 = (f32[5,16,8,128]{3,2,1,0:T(8,128)S(1)}, f32[3,16,8,128]{3,2,1,0:T(8,128)S(1)}) custom-call(s32[8,128]{1,0:T(8,128)S(1)} %reshape.7.depth_ref, f32[5,16,8,128]{3,2,1,0:T(8,128)S(1)} %copy-done.3, f32[8,16,8,128]{3,2,1,0:T(8,128)S(1)} %copy-done, f32[8,16,8,128]{3,2,1,0:T(8,128)S(1)} %copy-done.1, s32[8,16,8,128]{3,2,1,0:T(8,128)S(1)} %copy-done.2, ...), custom_call_target="tpu_custom_call" | custom-call | tf_op jit(solution)/shard_map/slab_step/pallas_call | solution.py:595
  52.8 0.7 %copy.12 = f32[5,16,8,128]{3,2,1,0:T(8,128)} copy(f32[5,16,8,128]{3,2,1,0:T(8,128)S(1)} %get-tuple-element.4) | data formatting | bytes 655360
  53.6 0.7 %copy.13 = f32[3,16,8,128]{3,2,1,0:T(8,128)} copy(f32[3,16,8,128]{3,2,1,0:T(8,128)S(1)} %get-tuple-element.5) | data formatting | bytes 393216
Async XLA Ops:
  0.6 1.0 %copy-start.4 = (s32[16,8,128]{2,1,0:T(8,128)S(1)}, s32[16,8,128]{2,1,0:T(8,128)}, u32[]{:S(2)}) copy-start(s32[16,8,128]{2,1,0:T(8,128)} %counts_hbm.1) | copy-start | bytes 196612
  1.6 1.0 %copy-start = (f32[8,16,8,128]{3,2,1,0:T(8,128)S(1)}, f32[8,16,8,128]{3,2,1,0:T(8,128)}, u32[]{:S(2)}) copy-start(f32[8,16,8,128]{3,2,1,0:T(8,128)} %radius_hbm.1) | copy-start | bytes 1572868
  2.7 1.0 %copy-start.1 = (f32[8,16,8,128]{3,2,1,0:T(8,128)S(1)}, f32[8,16,8,128]{3,2,1,0:T(8,128)}, u32[]{:S(2)}) copy-start(f32[8,16,8,128]{3,2,1,0:T(8,128)} %weight_hbm.1) | copy-start | bytes 1572868
  3.7 1.0 %copy-start.2 = (s32[8,16,8,128]{3,2,1,0:T(8,128)S(1)}, s32[8,16,8,128]{3,2,1,0:T(8,128)}, u32[]{:S(2)}) copy-start(s32[8,16,8,128]{3,2,1,0:T(8,128)} %column_hbm.1) | copy-start | bytes 1572868
  4.7 1.0 %copy-start.3 = (f32[5,16,8,128]{3,2,1,0:T(8,128)S(1)}, f32[5,16,8,128]{3,2,1,0:T(8,128)}, u32[]{:S(2)}) copy-start(f32[5,16,8,128]{3,2,1,0:T(8,128)} %fields_hbm.1) | copy-start | bytes 983044
